TPU v7x, 32 devices: a whole 2x2x4 slice. The times are simulated.
32 devices in a mesh: bank: 4 (over x, core), zero: 8 (over z, y).
Axes of the slice: x: 2, y: 2, z: 4, core: 2. Of those that a mesh axis runs over, the one named last changes fastest.
Arguments:
- train_gate: float32 [128, 2048, 768], P('bank', 'zero'), may hold values from -0.1875 to 0.1875
- other_gate: bfloat16 [128, 2048, 768], P('bank', 'zero'), may hold values from -0.0625 to 0.0625
- train_up: float32 [128, 2048, 768], P('bank', 'zero'), may hold values from -0.1875 to 0.1875
- other_up: bfloat16 [128, 2048, 768], P('bank', 'zero'), may hold values from -0.0625 to 0.0625
- router_weight: float32 [2048, 128], P('zero', 'bank'), may hold values from -0.125 to 0.125
- router_gain: float32 [2048], P('zero'), may hold values from 0.25 to 1.75
Outputs:
- ready_gate: bfloat16 [128, 2048, 768], P('bank', None, 'zero')
- ready_up: bfloat16 [128, 2048, 768], P('bank', None, 'zero')
- scale_gate: float32 [128, 768], P('bank', 'zero')
- scale_up: float32 [128, 768], P('bank', 'zero')
- serve_router: bfloat16 [2048, 128], replicated
All inputs are finite; a program needn't handle non-finite values. Where the computation divides by a largest or mean magnitude, that divisor is 1e-20 or more.
Results may differ from a plain program's by a relative error of at most 0.001.
Values may be sent and summed in bfloat16 or wider, within the bound.
No kernel may reach another device: no remote copies, remote signals or barrier semaphores. Data moves between devices by JAX's collectives and lax.ppermute only.
A program may use at most 256 MiB of HBM per device.

v0:
```python
import jax
import jax.numpy as jnp
from jax import lax
from jax.sharding import PartitionSpec as P


def on_device(train_gate, other_gate, train_up, other_up, router_weight, router_gain):
    latest_gate = train_gate + other_gate.astype(jnp.float32)
    latest_up = train_up + other_up.astype(jnp.float32)
    scale_gate, scale_up = lax.pmax(
        (jnp.max(jnp.abs(latest_gate), axis=1), jnp.max(jnp.abs(latest_up), axis=1)), "zero"
    )
    narrow_gate, narrow_up = (
        (latest_gate / jnp.expand_dims(scale_gate, 1)).astype(jnp.bfloat16),
        (latest_up / jnp.expand_dims(scale_up, 1)).astype(jnp.bfloat16),
    )
    ready_gate, ready_up = (
        lax.all_to_all(narrow_gate, "zero", split_axis=2, concat_axis=1, tiled=True),
        lax.all_to_all(narrow_up, "zero", split_axis=2, concat_axis=1, tiled=True),
    )
    scale_gate = lax.dynamic_slice_in_dim(
        scale_gate, lax.axis_index("zero") * ready_gate.shape[2], ready_gate.shape[2], axis=1
    )
    scale_up = lax.dynamic_slice_in_dim(
        scale_up, lax.axis_index("zero") * ready_up.shape[2], ready_up.shape[2], axis=1
    )
    part_router = (router_weight * router_gain[:, None]).astype(jnp.bfloat16)
    row_router = lax.all_gather(part_router, "zero", axis=0, tiled=True)
    serve_router = lax.all_gather(row_router, "bank", axis=1, tiled=True)
    return (ready_gate, ready_up, scale_gate, scale_up, serve_router)


def solution(mesh):
    return jax.shard_map(
        on_device,
        mesh=mesh,
        in_specs=(
            P("bank", "zero", None),
            P("bank", "zero", None),
            P("bank", "zero", None),
            P("bank", "zero", None),
            P("zero", "bank"),
            P("zero"),
        ),
        out_specs=(
            P("bank", None, "zero"),
            P("bank", None, "zero"),
            P("bank", "zero"),
            P("bank", "zero"),
            P(),
        ),
        check_vma=False,
    )
```

profile of v0, /device:TPU:0, one launch (start us, length us, event | category | flops | bytes accessed | tf_op | source)
XLA Modules:
  0.0 885.5 jit_solution(4941322030642369728)
XLA Ops:
  7.2 0.0 all-reduce.3.cloned.1.call-start
  7.2 25.0 %copy.42 = f32[32,256,768]{1,0,2:T(8,128)} copy(f32[32,256,768]{2,1,0:T(8,128)} %param.8) | data formatting | bytes 50331648 | tf_op args[2]
  32.2 16.9 %copy.41 = bf16[32,256,768]{1,0,2:T(8,128)(2,1)} copy(bf16[32,256,768]{2,1,0:T(8,128)(2,1)} %param.9) | data formatting | bytes 25165824 | tf_op args[3]
  49.1 25.0 %copy.38 = f32[32,256,768]{1,0,2:T(8,128)} copy(f32[32,256,768]{2,1,0:T(8,128)} %param.6) | data formatting | bytes 50331648 | tf_op args[0]
  74.2 16.9 %copy.37 = bf16[32,256,768]{1,0,2:T(8,128)(2,1)} copy(bf16[32,256,768]{2,1,0:T(8,128)(2,1)} %param.7) | data formatting | bytes 25165824 | tf_op args[1]
  91.0 0.0 copy-start
  91.0 14.4 %abs_reduce_fusion = f32[32,768]{0,1:T(8,128)} fusion(f32[32,256,768]{1,0,2:T(8,128)} %copy.42, bf16[32,256,768]{1,0,2:T(8,128)(2,1)} %copy.41), kind=kLoop, calls=%fused_computation.1 | loop fusion | flops 25141248 | bytes 37847040 | tf_op jit(solution)/shard_map/reduce_max | solution.py:11
  105.4 4.7 copy-done
  110.1 9.7 %abs_reduce_fusion.1 = f32[32,768]{0,1:T(8,128)} fusion(f32[32,256,768]{1,0,2:T(8,128)S(1)} %copy-done, bf16[32,256,768]{1,0,2:T(8,128)(2,1)} %copy.37), kind=kLoop, calls=%fused_computation.4 | loop fusion | flops 25141248 | bytes 37847040 | tf_op jit(solution)/shard_map/reduce_max | solution.py:11
  119.9 0.0 all-reduce.3.cloned.1.call-update
  119.9 78.2 %all-reduce.3.cloned.1.call-done = (f32[32,768]{0,1:T(8,128)}, f32[32,768]{0,1:T(8,128)}) async-done(((f32[32,768]{0,1:T(8,128)}, f32[32,768]{0,1:T(8,128)}), (f32[32,768]{0,1:T(8,128)}, f32[32,768]{0,1:T(8,128)})) %all-reduce.3.cloned.1.call-update) | async-done | bytes 196624 | tf_op jit(solution)/shard_map/pmax | solution.py:10
  198.1 29.4 %divide_convert_fusion = (bf16[32,256,768]{1,0,2:T(8,128)(2,1)}, bf16[32,256,768]{1,0,2:T(8,128)(2,1)S(1)}) fusion(f32[32,256,768]{1,0,2:T(8,128)} %copy.42, bf16[32,256,768]{1,0,2:T(8,128)(2,1)} %copy.41, f32[32,768]{0,1:T(8,128)} %get-tuple-element.16, f32[32,768]{0,1:T(8,128)} %get-tuple-element.15, f32[32,256,768]{1,0,2:T(8,128)} %copy.38, ...), kind=kLoop, calls=%fused_computation | loop fusion | flops 50331648 | bytes 100859904 | tf_op jit(solution)/shard_map/convert_element_type | solution.py:15
  227.5 0.0 copy-start.1
  227.6 0.0 copy-start.2
  227.6 276.4 %all_to_all.36 = bf16[32,256,768]{1,0,2:T(8,128)(2,1)} all-to-all(bf16[32,256,768]{1,0,2:T(8,128)(2,1)S(1)} %get-tuple-element.18), channel_id=1, replica_groups=mesh['bank'=4,'zero'=8] {'zero'}, dimensions={2} | all-to-all | bytes 25165824 | tf_op jit(solution)/shard_map/all_to_all | solution.py:18
  504.0 5.4 all-to-all-start.1
  509.3 0.0 copy-done.1
  509.4 0.0 copy-done.2
  509.4 292.0 %all_gather.6 = bf16[2048,32]{0,1:T(8,128)(2,1)S(1)} all-gather(bf16[256,32]{0,1:T(8,128)(2,1)S(1)} %multiply_convert_fusion), channel_id=1, replica_groups=mesh['bank'=4,'zero'=8] {'zero'}, dimensions={0}, use_global_device_ids=true | all-gather | bytes 147456 | tf_op jit(solution)/shard_map/all_gather | solution.py:28
  801.4 7.0 all_gather.7
  808.4 1.0 copy.47
  809.4 0.8 constant_dynamic-slice_fusion
  810.2 0.7 copy.45
  810.9 0.7 copy.46
  811.6 14.1 %copy.40 = bf16[32,8,256,96]{2,1,3,0:T(8,128)(2,1)} copy(bf16[32,8,256,96]{2,0,3,1:T(8,128)(2,1)} %bitcast.14) | data formatting | bytes 25165824 | tf_op jit(solution)/shard_map/all_to_all | solution.py:18
  825.6 19.5 %all_to_all.29 = bf16[32,2048,96]{1,2,0:T(8,128)(2,1)} reshape(bf16[32,8,256,96]{2,1,3,0:T(8,128)(2,1)} %copy.40) | data formatting | bytes 25165824 | tf_op jit(solution)/shard_map/all_to_all | solution.py:18
  845.1 0.0 all-to-all-done.1
  845.1 14.1 %copy.44 = bf16[32,8,256,96]{2,1,3,0:T(8,128)(2,1)} copy(bf16[32,8,256,96]{2,0,3,1:T(8,128)(2,1)} %bitcast.5) | data formatting | bytes 25165824 | tf_op jit(solution)/shard_map/all_to_all | solution.py:19
  859.2 19.5 %all_to_all.33 = bf16[32,2048,96]{1,2,0:T(8,128)(2,1)} reshape(bf16[32,8,256,96]{2,1,3,0:T(8,128)(2,1)} %copy.44) | data formatting | bytes 25165824 | tf_op jit(solution)/shard_map/all_to_all | solution.py:19
  (1 shorter events, 0.0 us)
Async XLA Ops:
  7.2 191.0 %all-reduce.3.cloned.1.call-start = ((), (), s32[]{:S(2)}) async-start(), calls=%async_computation.2 | async-start | bytes 1572864 | tf_op jit(solution)/shard_map/pmax | solution.py:10
  91.0 19.1 %copy-start = (f32[32,256,768]{1,0,2:T(8,128)S(1)}, f32[32,256,768]{1,0,2:T(8,128)}, u32[]{:S(2)}) copy-start(f32[32,256,768]{1,0,2:T(8,128)} %copy.38) | copy-start | bytes 75497472
  227.5 281.8 %copy-start.1 = (f32[256,32]{0,1:T(8,128)S(1)}, f32[256,32]{0,1:T(8,128)}, u32[]{:S(2)}) copy-start(f32[256,32]{0,1:T(8,128)} %param.10) | copy-start | bytes 98308
  227.6 281.8 %copy-start.2 = (f32[256]{0:T(256)S(1)}, f32[256]{0:T(256)}, u32[]{:S(2)}) copy-start(f32[256]{0:T(256)} %param.11) | copy-start | bytes 3076
  504.0 341.1 %all-to-all-start.1 = ((bf16[32,256,768]{1,0,2:T(8,128)(2,1)}), bf16[32,256,768]{1,0,2:T(8,128)(2,1)}, u32[]{:S(2)}, u32[]{:S(2)}) async-start(bf16[32,256,768]{1,0,2:T(8,128)(2,1)} %get-tuple-element.17), calls=%async_computation.1 | async-start | bytes 25165824 | tf_op jit(solution)/shard_map/all_to_all | solution.py:19
Sparse Core Ops, SparseCore 0:
  120.0 78.0 all-reduce.2
where the time goes:
time: 889 us; the launch traced here: 886 us
  blocking collectives  575 us (65%)
  local copies, waits for them, and re-layouts  159 us (18%)
  waiting for transfers between devices  78.2 us (9%)
  other arithmetic  53.5 us (6%)
  between operations  14.1 us (2%)
    all_gather x1, blocking collectives, on_device(): row_router = lax.all_gather(part_router, 'zero', axis=0, tiled=True)  292 us
    all_to_all x1, blocking collectives, on_device(): lax.all_to_all(narrow_gate, 'zero', split_axis=2, concat_axis=1, tiled=True)  276 us
    unnamed x13, local copies, waits for them, and re-layouts  90.9 us
    pmax x1, waiting for transfers between devices, on_device(): lax.pmax((jnp.max(jnp.abs(latest_gate), axis=1), jnp.max(jnp.abs(latest_u...  78.2 us
    all_to_all x2, local copies, waits for them, and re-layouts, on_device(): lax.all_to_all(narrow_gate, 'zero', split_axis=2, concat_axis=1, tiled=True)  33.5 us
    all_to_all x2, local copies, waits for them, and re-layouts, on_device(): lax.all_to_all(narrow_up, 'zero', split_axis=2, concat_axis=1, tiled=True)  33.5 us
    convert_element_type x1, other arithmetic, on_device(): (latest_up / jnp.expand_dims(scale_up, 1)).astype(jnp.bfloat16)  29.4 us
  transfers between devices with their start and end apart: 2, of which 1 were waited for; matrix products, arithmetic and copies ran while one was open for 2% of the time, Pallas kernels for 0%

commit v1 on v0

--- a/solution.py
+++ b/solution.py
@@ -15,7 +15,12 @@
         (latest_up / jnp.expand_dims(scale_up, 1)).astype(jnp.bfloat16),
     )
     ready_gate, ready_up = (
-        lax.all_to_all(narrow_gate, "zero", split_axis=2, concat_axis=1, tiled=True),
+        jnp.concatenate(
+            lax.all_to_all(
+                jnp.stack(jnp.split(narrow_gate, lax.axis_size("zero"), axis=2)), "zero", 0, 0
+            ),
+            axis=1,
+        ),
         lax.all_to_all(narrow_up, "zero", split_axis=2, concat_axis=1, tiled=True),
     )
     scale_gate = lax.dynamic_slice_in_dim(

time: 889 us -> 856 us (0.963)
  blocking collectives: 575 us -> 299 us
  waiting for transfers between devices: 78.2 us -> 330 us
  local copies, waits for them, and re-layouts: 159 us -> 145 us
    all_to_all x1 -> x0, blocking collectives: 276 us -> none  [on_device(): lax.all_to_all(narrow_gate, 'zero', split_axis=2, concat_axis=1, tiled=True)]
    all_to_all x0 -> x1, waiting for transfers between devices: none -> 254 us  [on_device(): lax.all_to_all(jnp.stack(jnp.split(narrow_gate, lax.axis_size('zero'), ax...]
    all_to_all x2 -> x0, local copies, waits for them, and re-layouts: 33.5 us -> none  [on_device(): lax.all_to_all(narrow_gate, 'zero', split_axis=2, concat_axis=1, tiled=True)]
    convert_element_type x0 -> x1, other arithmetic: none -> 12.9 us  [on_device(): (latest_gate / jnp.expand_dims(scale_gate, 1)).astype(jnp.bfloat16)]
    convert_element_type x1, other arithmetic: 29.4 us -> 16.9 us  [on_device(): (latest_up / jnp.expand_dims(scale_up, 1)).astype(jnp.bfloat16)]
    reshape x0 -> x1, local copies, waits for them, and re-layouts: none -> 10.9 us  [on_device(): jnp.concatenate(lax.all_to_all(jnp.stack(jnp.split(narrow_gate, lax.axis_...]
    unnamed x13 -> x21, local copies, waits for them, and re-layouts: 90.9 us -> 98.3 us
  transfers between devices with their start and end apart: 2 -> 3, of which waited for: 1 -> 2; matrix products, arithmetic and copies ran while one was open for 2% -> 4% of each run, Pallas kernels for 0% -> 0%
where the time goes in v1:
time: 856 us; the launch traced here: 853 us
  waiting for transfers between devices  330 us (39%)
  blocking collectives  299 us (35%)
  local copies, waits for them, and re-layouts  145 us (17%)
  other arithmetic  53.9 us (6%)
  between operations  14.1 us (2%)
  starting transfers between devices  10.9 us (1%)
    all_gather x1, blocking collectives, on_device(): row_router = lax.all_gather(part_router, 'zero', axis=0, tiled=True)  292 us
    all_to_all x1, waiting for transfers between devices, on_device(): lax.all_to_all(jnp.stack(jnp.split(narrow_gate, lax.axis_size('zero'), ax...  254 us
    unnamed x21, local copies, waits for them, and re-layouts  98.3 us
    pmax x1, waiting for transfers between devices, on_device(): lax.pmax((jnp.max(jnp.abs(latest_gate), axis=1), jnp.max(jnp.abs(latest_u...  76 us
    all_to_all x2, local copies, waits for them, and re-layouts, on_device(): lax.all_to_all(narrow_up, 'zero', split_axis=2, concat_axis=1, tiled=True)  33.6 us
  transfers between devices with their start and end apart: 3, of which 2 were waited for; matrix products, arithmetic and copies ran while one was open for 4% of the time, Pallas kernels for 0%

profile of v1, /device:TPU:0, one launch (start us, length us, event | category | flops | bytes accessed | tf_op | source)
XLA Modules:
  0.0 853.4 jit_solution(17380871487517755548)
XLA Ops:
  7.2 0.0 all-reduce.3.cloned.1.call-start
  7.2 25.1 %copy.44 = f32[32,256,768]{1,0,2:T(8,128)} copy(f32[32,256,768]{2,1,0:T(8,128)} %param.8) | data formatting | bytes 50331648 | tf_op args[2]
  32.3 16.9 %copy.43 = bf16[32,256,768]{1,0,2:T(8,128)(2,1)} copy(bf16[32,256,768]{2,1,0:T(8,128)(2,1)} %param.9) | data formatting | bytes 25165824 | tf_op args[3]
  49.2 24.6 %copy.41 = f32[32,256,768]{1,2,0:T(8,128)} copy(f32[32,256,768]{2,1,0:T(8,128)} %param.6) | data formatting | bytes 50331648 | tf_op args[0]
  73.8 16.6 %copy.40 = bf16[32,256,768]{1,2,0:T(8,128)(2,1)} copy(bf16[32,256,768]{2,1,0:T(8,128)(2,1)} %param.7) | data formatting | bytes 25165824 | tf_op args[1]
  90.4 14.3 %abs_reduce_fusion = f32[32,768]{0,1:T(8,128)} fusion(f32[32,256,768]{1,0,2:T(8,128)} %copy.44, bf16[32,256,768]{1,0,2:T(8,128)(2,1)} %copy.43), kind=kLoop, calls=%fused_computation.1 | loop fusion | flops 25141248 | bytes 37847040 | tf_op jit(solution)/shard_map/reduce_max | solution.py:11
  104.7 4.8 copy-done
  109.5 9.7 %abs_reduce_fusion.1 = f32[32,768]{1,0:T(8,128)} fusion(f32[32,256,768]{1,2,0:T(8,128)S(1)} %copy-done, bf16[32,256,768]{1,2,0:T(8,128)(2,1)} %copy.40), kind=kLoop, calls=%fused_computation.4 | loop fusion | flops 25141248 | bytes 37847040 | tf_op jit(solution)/shard_map/reduce_max | solution.py:11
  119.2 0.0 all-reduce.3.cloned.1.call-update
  119.2 76.0 %all-reduce.3.cloned.1.call-done = (f32[32,768]{1,0:T(8,128)}, f32[32,768]{0,1:T(8,128)}) async-done(((f32[32,768]{1,0:T(8,128)}, f32[32,768]{0,1:T(8,128)}), (f32[32,768]{1,0:T(8,128)}, f32[32,768]{0,1:T(8,128)})) %all-reduce.3.cloned.1.call-update) | async-done | bytes 196624 | tf_op jit(solution)/shard_map/pmax | solution.py:10
  195.3 12.9 %divide_convert_fusion.1 = bf16[32,256,768]{1,2,0:T(8,128)(2,1)S(1)} fusion(f32[32,256,768]{1,2,0:T(8,128)} %copy.41, bf16[32,256,768]{1,2,0:T(8,128)(2,1)} %copy.40, f32[32,768]{1,0:T(8,128)} %get-tuple-element.20), kind=kLoop, calls=%fused_computation.3 | loop fusion | flops 25165824 | bytes 50429952 | tf_op jit(solution)/shard_map/convert_element_type | solution.py:14
  208.1 1.2 fusion.7
  209.4 1.2 fusion.6
  210.6 1.2 fusion.5
  211.9 1.2 fusion.4
  213.1 1.2 fusion.3
  214.4 1.2 fusion.2
  215.6 1.2 fusion.1
  216.8 1.2 fusion
  218.1 5.5 all-to-all-start
  223.7 16.9 %divide_convert_fusion = bf16[32,256,768]{1,0,2:T(8,128)(2,1)} fusion(f32[32,256,768]{1,0,2:T(8,128)} %copy.44, bf16[32,256,768]{1,0,2:T(8,128)(2,1)} %copy.43, f32[32,768]{0,1:T(8,128)S(1)} %copy-done.1), kind=kLoop, calls=%fused_computation | loop fusion | flops 25165824 | bytes 50429952 | tf_op jit(solution)/shard_map/convert_element_type | solution.py:15
  240.6 254.3 %all-to-all-done = bf16[8,32,256,96]{2,3,1,0:T(8,128)(2,1)} async-done(((bf16[8,32,256,96]{2,3,1,0:T(8,128)(2,1)}), bf16[8,32,256,96]{2,3,1,0:T(8,128)(2,1)}, u32[]{:S(2)}, u32[]{:S(2)}) %all-to-all-start) | async-done | bytes 12582944 | tf_op jit(solution)/shard_map/all_to_all | solution.py:19
  494.9 5.4 all-to-all-start.1
  500.3 291.6 %all_gather.6 = bf16[2048,32]{0,1:T(8,128)(2,1)S(1)} all-gather(bf16[256,32]{0,1:T(8,128)(2,1)S(1)} %multiply_convert_fusion), channel_id=1, replica_groups=mesh['bank'=4,'zero'=8] {'zero'}, dimensions={0}, use_global_device_ids=true | all-gather | bytes 147456 | tf_op jit(solution)/shard_map/all_gather | solution.py:33
  791.9 7.1 all_gather.7
  799.0 1.0 copy.48
  800.1 0.7 copy.47
  800.7 1.4 constant_dynamic-slice_fusion.1
  802.2 10.9 %copy.50 = bf16[8,32,12,8,256]{4,3,0,2,1:T(8,128)(2,1)} copy(bf16[8,32,12,8,256]{4,3,2,1,0:T(8,128)(2,1)} %bitcast.12) | data formatting | bytes 25165824 | tf_op jit(solution)/shard_map/reshape | solution.py:18
  813.0 0.0 all-to-all-done.1
  813.0 14.1 %copy.46 = bf16[32,8,256,96]{2,1,3,0:T(8,128)(2,1)} copy(bf16[32,8,256,96]{2,0,3,1:T(8,128)(2,1)} %bitcast.11) | data formatting | bytes 25165824 | tf_op jit(solution)/shard_map/all_to_all | solution.py:24
  827.1 19.5 %all_to_all.20 = bf16[32,2048,96]{1,2,0:T(8,128)(2,1)} reshape(bf16[32,8,256,96]{2,1,3,0:T(8,128)(2,1)} %copy.46) | data formatting | bytes 25165824 | tf_op jit(solution)/shard_map/all_to_all | solution.py:24
  (9 shorter events, 0.0 us)
Async XLA Ops:
  7.2 188.1 %all-reduce.3.cloned.1.call-start = ((), (), s32[]{:S(2)}) async-start(), calls=%async_computation.2 | async-start | bytes 983040 | tf_op jit(solution)/shard_map/pmax | solution.py:10
  90.4 19.1 %copy-start = (f32[32,256,768]{1,2,0:T(8,128)S(1)}, f32[32,256,768]{1,2,0:T(8,128)}, u32[]{:S(2)}) copy-start(f32[32,256,768]{1,2,0:T(8,128)} %copy.41) | copy-start | bytes 75497472
  218.1 5.6 copy-start.1
  218.1 276.8 %all-to-all-start = ((bf16[8,32,256,96]{2,3,1,0:T(8,128)(2,1)}), bf16[8,32,256,96]{2,3,1,0:T(8,128)(2,1)}, u32[]{:S(2)}, u32[]{:S(2)}) async-start(bf16[8,32,256,96]{2,3,1,0:T(8,128)(2,1)} %fusion), calls=%async_computation | async-start | bytes 25165824 | tf_op jit(solution)/shard_map/all_to_all | solution.py:19
  240.6 259.7 %copy-start.2 = (f32[256,32]{0,1:T(8,128)S(1)}, f32[256,32]{0,1:T(8,128)}, u32[]{:S(2)}) copy-start(f32[256,32]{0,1:T(8,128)} %param.10) | copy-start | bytes 98308
  240.6 259.7 %copy-start.3 = (f32[256]{0:T(256)S(1)}, f32[256]{0:T(256)}, u32[]{:S(2)}) copy-start(f32[256]{0:T(256)} %param.11) | copy-start | bytes 3076
  494.9 318.1 %all-to-all-start.1 = ((bf16[32,256,768]{1,0,2:T(8,128)(2,1)}), bf16[32,256,768]{1,0,2:T(8,128)(2,1)}, u32[]{:S(2)}, u32[]{:S(2)}) async-start(bf16[32,256,768]{1,0,2:T(8,128)(2,1)} %divide_convert_fusion), calls=%async_computation.1 | async-start | bytes 25165824 | tf_op jit(solution)/shard_map/all_to_all | solution.py:24
Sparse Core Ops, SparseCore 0:
  119.4 75.8 all-reduce.2

commit v2 on v0

--- a/solution.py
+++ b/solution.py
@@ -26,7 +26,7 @@
     )
     part_router = (router_weight * router_gain[:, None]).astype(jnp.bfloat16)
     row_router = lax.all_gather(part_router, "zero", axis=0, tiled=True)
-    serve_router = lax.all_gather(row_router, "bank", axis=1, tiled=True)
+    serve_router = jnp.concatenate(lax.all_gather(row_router, "bank"), axis=1)
     return (ready_gate, ready_up, scale_gate, scale_up, serve_router)
 
 

time: 889 us -> 889 us (level)
  no operation moved by 1% of the time
where the time goes in v2:
time: 889 us; the launch traced here: 886 us
  blocking collectives  575 us (65%)
  local copies, waits for them, and re-layouts  160 us (18%)
  waiting for transfers between devices  78.2 us (9%)
  other arithmetic  53.5 us (6%)
  between operations  14.1 us (2%)
    all_gather x1, blocking collectives, on_device(): row_router = lax.all_gather(part_router, 'zero', axis=0, tiled=True)  292 us
    all_to_all x1, blocking collectives, on_device(): lax.all_to_all(narrow_gate, 'zero', split_axis=2, concat_axis=1, tiled=True)  276 us
    unnamed x13, local copies, waits for them, and re-layouts  90.9 us
    pmax x1, waiting for transfers between devices, on_device(): lax.pmax((jnp.max(jnp.abs(latest_gate), axis=1), jnp.max(jnp.abs(latest_u...  78.2 us
    all_to_all x2, local copies, waits for them, and re-layouts, on_device(): lax.all_to_all(narrow_gate, 'zero', split_axis=2, concat_axis=1, tiled=True)  33.5 us
    all_to_all x2, local copies, waits for them, and re-layouts, on_device(): lax.all_to_all(narrow_up, 'zero', split_axis=2, concat_axis=1, tiled=True)  33.5 us
    convert_element_type x1, other arithmetic, on_device(): (latest_up / jnp.expand_dims(scale_up, 1)).astype(jnp.bfloat16)  29.4 us
  transfers between devices with their start and end apart: 2, of which 1 were waited for; matrix products, arithmetic and copies ran while one was open for 2% of the time, Pallas kernels for 0%

profile of v2, /device:TPU:0, one launch (start us, length us, event | category | flops | bytes accessed | tf_op | source)
XLA Modules:
  0.0 886.2 jit_solution(148892652662324902)
XLA Ops:
  7.2 0.0 all-reduce.3.cloned.1.call-start
  7.2 25.0 %copy.44 = f32[32,256,768]{1,0,2:T(8,128)} copy(f32[32,256,768]{2,1,0:T(8,128)} %param.8) | data formatting | bytes 50331648 | tf_op args[2]
  32.2 16.9 %copy.43 = bf16[32,256,768]{1,0,2:T(8,128)(2,1)} copy(bf16[32,256,768]{2,1,0:T(8,128)(2,1)} %param.9) | data formatting | bytes 25165824 | tf_op args[3]
  49.1 25.0 %copy.40 = f32[32,256,768]{1,0,2:T(8,128)} copy(f32[32,256,768]{2,1,0:T(8,128)} %param.6) | data formatting | bytes 50331648 | tf_op args[0]
  74.2 16.9 %copy.39 = bf16[32,256,768]{1,0,2:T(8,128)(2,1)} copy(bf16[32,256,768]{2,1,0:T(8,128)(2,1)} %param.7) | data formatting | bytes 25165824 | tf_op args[1]
  91.0 0.0 copy-start
  91.0 14.4 %abs_reduce_fusion = f32[32,768]{0,1:T(8,128)} fusion(f32[32,256,768]{1,0,2:T(8,128)} %copy.44, bf16[32,256,768]{1,0,2:T(8,128)(2,1)} %copy.43), kind=kLoop, calls=%fused_computation.1 | loop fusion | flops 25141248 | bytes 37847040 | tf_op jit(solution)/shard_map/reduce_max | solution.py:11
  105.4 4.7 copy-done
  110.1 9.7 %abs_reduce_fusion.1 = f32[32,768]{0,1:T(8,128)} fusion(f32[32,256,768]{1,0,2:T(8,128)S(1)} %copy-done, bf16[32,256,768]{1,0,2:T(8,128)(2,1)} %copy.39), kind=kLoop, calls=%fused_computation.4 | loop fusion | flops 25141248 | bytes 37847040 | tf_op jit(solution)/shard_map/reduce_max | solution.py:11
  119.9 0.0 all-reduce.3.cloned.1.call-update
  119.9 78.2 %all-reduce.3.cloned.1.call-done = (f32[32,768]{0,1:T(8,128)}, f32[32,768]{0,1:T(8,128)}) async-done(((f32[32,768]{0,1:T(8,128)}, f32[32,768]{0,1:T(8,128)}), (f32[32,768]{0,1:T(8,128)}, f32[32,768]{0,1:T(8,128)})) %all-reduce.3.cloned.1.call-update) | async-done | bytes 196624 | tf_op jit(solution)/shard_map/pmax | solution.py:10
  198.1 29.4 %divide_convert_fusion = (bf16[32,256,768]{1,0,2:T(8,128)(2,1)}, bf16[32,256,768]{1,0,2:T(8,128)(2,1)S(1)}) fusion(f32[32,256,768]{1,0,2:T(8,128)} %copy.44, bf16[32,256,768]{1,0,2:T(8,128)(2,1)} %copy.43, f32[32,768]{0,1:T(8,128)} %get-tuple-element.26, f32[32,768]{0,1:T(8,128)} %get-tuple-element.25, f32[32,256,768]{1,0,2:T(8,128)} %copy.40, ...), kind=kLoop, calls=%fused_computation | loop fusion | flops 50331648 | bytes 100859904 | tf_op jit(solution)/shard_map/convert_element_type | solution.py:15
  227.5 0.0 copy-start.1
  227.6 0.0 copy-start.2
  227.6 276.4 %all_to_all.36 = bf16[32,256,768]{1,0,2:T(8,128)(2,1)} all-to-all(bf16[32,256,768]{1,0,2:T(8,128)(2,1)S(1)} %get-tuple-element.28), channel_id=1, replica_groups=mesh['bank'=4,'zero'=8] {'zero'}, dimensions={2} | all-to-all | bytes 25165824 | tf_op jit(solution)/shard_map/all_to_all | solution.py:18
  504.0 5.4 all-to-all-start.1
  509.3 0.0 copy-done.1
  509.4 0.0 copy-done.2
  509.4 292.0 %all_gather.9 = bf16[2048,32]{0,1:T(8,128)(2,1)S(1)} all-gather(bf16[256,32]{0,1:T(8,128)(2,1)S(1)} %multiply_convert_fusion), channel_id=1, replica_groups=mesh['bank'=4,'zero'=8] {'zero'}, dimensions={0}, use_global_device_ids=true | all-gather | bytes 147456 | tf_op jit(solution)/shard_map/all_gather | solution.py:28
  801.4 7.0 all-gather
  808.4 0.4 reshape.21
  808.8 0.3 copy.47
  809.1 1.0 copy.50
  810.1 0.8 constant_dynamic-slice_fusion
  810.9 0.7 copy.48
  811.6 0.7 copy.49
  812.3 14.1 %copy.42 = bf16[32,8,256,96]{2,1,3,0:T(8,128)(2,1)} copy(bf16[32,8,256,96]{2,0,3,1:T(8,128)(2,1)} %bitcast.18) | data formatting | bytes 25165824 | tf_op jit(solution)/shard_map/all_to_all | solution.py:18
  826.3 19.5 %all_to_all.29 = bf16[32,2048,96]{1,2,0:T(8,128)(2,1)} reshape(bf16[32,8,256,96]{2,1,3,0:T(8,128)(2,1)} %copy.42) | data formatting | bytes 25165824 | tf_op jit(solution)/shard_map/all_to_all | solution.py:18
  845.8 0.0 all-to-all-done.1
  845.8 14.1 %copy.46 = bf16[32,8,256,96]{2,1,3,0:T(8,128)(2,1)} copy(bf16[32,8,256,96]{2,0,3,1:T(8,128)(2,1)} %bitcast.5) | data formatting | bytes 25165824 | tf_op jit(solution)/shard_map/all_to_all | solution.py:19
  859.9 19.5 %all_to_all.33 = bf16[32,2048,96]{1,2,0:T(8,128)(2,1)} reshape(bf16[32,8,256,96]{2,1,3,0:T(8,128)(2,1)} %copy.46) | data formatting | bytes 25165824 | tf_op jit(solution)/shard_map/all_to_all | solution.py:19
  (1 shorter events, 0.0 us)
Async XLA Ops:
  7.2 191.0 %all-reduce.3.cloned.1.call-start = ((), (), s32[]{:S(2)}) async-start(), calls=%async_computation.2 | async-start | bytes 1572864 | tf_op jit(solution)/shard_map/pmax | solution.py:10
  91.0 19.1 %copy-start = (f32[32,256,768]{1,0,2:T(8,128)S(1)}, f32[32,256,768]{1,0,2:T(8,128)}, u32[]{:S(2)}) copy-start(f32[32,256,768]{1,0,2:T(8,128)} %copy.40) | copy-start | bytes 75497472
  227.5 281.8 %copy-start.1 = (f32[256,32]{0,1:T(8,128)S(1)}, f32[256,32]{0,1:T(8,128)}, u32[]{:S(2)}) copy-start(f32[256,32]{0,1:T(8,128)} %param.10) | copy-start | bytes 98308
  227.6 281.8 %copy-start.2 = (f32[256]{0:T(256)S(1)}, f32[256]{0:T(256)}, u32[]{:S(2)}) copy-start(f32[256]{0:T(256)} %param.11) | copy-start | bytes 3076
  504.0 341.8 %all-to-all-start.1 = ((bf16[32,256,768]{1,0,2:T(8,128)(2,1)}), bf16[32,256,768]{1,0,2:T(8,128)(2,1)}, u32[]{:S(2)}, u32[]{:S(2)}) async-start(bf16[32,256,768]{1,0,2:T(8,128)(2,1)} %get-tuple-element.27), calls=%async_computation.1 | async-start | bytes 25165824 | tf_op jit(solution)/shard_map/all_to_all | solution.py:19
Sparse Core Ops, SparseCore 0:
  120.0 78.0 all-reduce.2
